TPU v7x, 32 devices: a whole 2x2x4 slice. The times are simulated.
32 devices in a mesh: row: 4 (over y, x), col: 4 (over z), dep: 2 (over core).
Axes of the slice: x: 2, y: 2, z: 4, core: 2. Of those that a mesh axis runs over, the one named last changes fastest.
Arguments:
- matrix: float32 [16384, 16384], P('row', ('col', 'dep')), may hold values from -6 to 6
- vectors: float32 [64, 16384], P(None, ('row', 'col')), may hold values from -0.09375 to 0.09375
Outputs:
- reduced: float32 [16384, 16384], P('row', ('col', 'dep'))
All inputs are finite; a program needn't handle non-finite values.
Results may differ from a plain program's by a relative error of at most 0.0001.
Values sent between devices are 32-bit elements; how exact they have to be, the bound alone decides.
A program may use at most 128 MiB of HBM per device.

v0:
```python
import jax
import jax.numpy as jnp
from jax import lax
from jax.sharding import PartitionSpec as P

highest = lax.Precision.HIGHEST


def broadcast(value, axis, source):
    kept = jnp.where(lax.axis_index(axis) == source, value, 0).astype(value.dtype)
    return lax.psum(kept, axis)


def contract(left, right, dims):
    return lax.dot_general(left, right, (dims, ((), ())), precision=highest)


def mask_vectors(values, first_row):
    panel_width, row_count = values.shape
    positions = first_row + lax.iota(jnp.int32, row_count)[None, :]
    reflector = lax.iota(jnp.int32, panel_width)[:, None]
    filler = jnp.where(positions == reflector + 1, 1.0, 0.0).astype(values.dtype)
    return jnp.where(positions > reflector + 1, values, filler)


def make_factor(gram):
    size_b = gram.shape[0]
    half_diag = 0.5 * jnp.diagonal(gram)
    scaled = jnp.triu(gram, 1) / half_diag[:, None]
    identity = jnp.eye(size_b, dtype=gram.dtype)
    inverse = identity - scaled
    powered = scaled
    for level in range((size_b - 1).bit_length() - 1):
        powered = jnp.dot(powered, powered, precision=highest)
        inverse = jnp.dot(inverse, identity + powered, precision=highest)
    return inverse / half_diag[None, :]


def on_device(matrix, vectors):
    rows_dev, cols_dev = matrix.shape
    row_index = lax.axis_index("row")
    gathered = lax.all_gather(vectors, "col", axis=1, tiled=True)
    row_vectors = mask_vectors(gathered, row_index * rows_dev)
    col_block = lax.axis_index("col") * lax.axis_size("dep") + lax.axis_index("dep")
    offset = col_block * cols_dev - row_index * rows_dev
    local_piece = lax.dynamic_slice_in_dim(row_vectors, offset, cols_dev, 1)
    owner_row = col_block * cols_dev // rows_dev
    col_vectors = broadcast(local_piece, "row", owner_row)
    gram_part = contract(row_vectors, row_vectors, ((1,), (1,)))
    first_part = contract(row_vectors, matrix, ((1,), (0,)))
    gram_total, first_total = lax.psum((gram_part, first_part), "row")
    factor = make_factor(gram_total)
    partial_value = contract(col_vectors, matrix, ((1,), (1,)))
    summed = lax.psum(partial_value, ("col", "dep"))
    update = contract(factor, summed, ((0,), (0,)))
    cross_term = lax.psum(contract(row_vectors, update, ((1,), (1,))), "row")
    left_terms = first_total - jnp.dot(cross_term, col_vectors, precision=highest)
    scaled_terms = contract(factor, left_terms, ((0,), (0,)))
    stacked_left = jnp.concatenate([update, row_vectors], axis=0)
    stacked_right = jnp.concatenate([col_vectors, scaled_terms], axis=0)
    return matrix - contract(stacked_left, stacked_right, ((0,), (0,)))


def solution(mesh):
    placed = (P("row", ("col", "dep")), P(None, ("row", "col")))
    return jax.shard_map(
        on_device, mesh=mesh, in_specs=placed, out_specs=P("row", ("col", "dep")), check_vma=False
    )
```

profile of v0, /device:TPU:0, one launch (start us, length us, event | category | flops | bytes accessed | tf_op | source)
XLA Modules:
  0.0 297.8 jit_solution(16607201885257769943)
XLA Ops:
  6.5 0.0 all-gather.2.cloned.1.call-start
  6.5 0.7 all-gather.2.cloned.1.call-update
  7.3 0.0 all-reduce.6.cloned.1.call-start
  7.4 32.3 %all-gather.2.cloned.1.call-done = f32[64,4096]{1,0:T(8,128)} async-done(((f32[64,1024]{1,0:T(8,128)}), f32[64,4096]{1,0:T(8,128)}) %all-gather.2.cloned.1.call-update) | async-done | bytes 1048592 | tf_op jit(solution)/shard_map/all_gather | solution.py:42
  39.6 1.4 select_select_fusion
  41.1 1.0 fusion.14
  42.0 16.2 %psum.35 = f32[64,64]{1,0:T(8,128)S(1)} all-reduce(f32[64,64]{1,0:T(8,128)S(1)} %fusion.14), channel_id=1, replica_groups=mesh['row'=4,'col'=4,'dep'=2] {'row'}, use_global_device_ids=true, to_apply=%region_0.1 | all-reduce | flops 4096 | bytes 32768 | tf_op jit(solution)/shard_map/psum | solution.py:51
  58.3 0.8 gather_fusion
  59.1 0.2 fusion.10
  59.4 0.2 fusion.15
  59.5 24.8 %fusion.20 = f32[64,2048]{1,0:T(8,128)} fusion(f32[64,4096]{1,0:T(8,128)S(1)} %select_select_fusion, f32[4096,2048]{1,0:T(8,128)} %param.2), kind=kOutput, calls=%fused_computation.39 | convolution fusion | flops 6442450944 | bytes 35127296 | tf_op jit(solution)/shard_map/dot_general | solution.py:15
  84.3 0.8 dynamic-slice_select_fusion
  85.2 0.0 all-reduce.6.cloned.1.call-update
  85.2 0.2 all-reduce.4.cloned.1.call-start
  85.4 0.2 fusion.16
  85.6 0.2 fusion.6
  85.8 0.2 fusion.7
  86.0 0.2 fusion.17
  86.2 0.2 fusion.8
  86.3 49.1 %all-reduce.6.cloned.1.call-done = (f32[64,2048]{1,0:T(8,128)}, f32[64,2048]{1,0:T(8,128)}) async-done(((f32[64,2048]{1,0:T(8,128)}, f32[64,2048]{1,0:T(8,128)}), (f32[64,2048]{1,0:T(8,128)}, f32[64,2048]{1,0:T(8,128)})) %all-reduce.6.cloned.1.call-update) | async-done | bytes 1048592 | tf_op jit(solution)/shard_map/psum | solution.py:11
  135.4 0.0 copy-start
  135.4 0.0 copy-start.1
  135.4 42.8 %fusion.18 = f32[64,4096]{1,0:T(8,128)} fusion(f32[64,2048]{1,0:T(8,128)} %get-tuple-element.5, f32[4096,2048]{1,0:T(8,128)} %param.2), kind=kOutput, calls=%fused_computation.37 | convolution fusion | flops 6442450944 | bytes 35127296 | tf_op jit(solution)/shard_map/dot_general | solution.py:15
  178.3 0.0 all-reduce.4.cloned.1.call-update
  178.3 0.2 convolution_add_fusion
  178.5 0.2 fusion.9
  178.6 0.2 convolution_divide_fusion
  178.8 59.0 %all-reduce.4.cloned.1.call-done = f32[64,4096]{1,0:T(8,128)} async-done(((f32[64,4096]{1,0:T(8,128)}), f32[64,4096]{1,0:T(8,128)}) %all-reduce.4.cloned.1.call-update) | async-done | bytes 1048592 | tf_op jit(solution)/shard_map/psum | solution.py:54
  237.8 2.2 fusion.19
  240.0 1.0 fusion.21
  241.0 16.2 %psum.39 = f32[64,64]{1,0:T(8,128)S(1)} all-reduce(f32[64,64]{1,0:T(8,128)S(1)} %fusion.21), channel_id=1, replica_groups=mesh['row'=4,'col'=4,'dep'=2] {'row'}, use_global_device_ids=true, to_apply=%region_4.5 | all-reduce | flops 4096 | bytes 32768 | tf_op jit(solution)/shard_map/psum | solution.py:56
  257.2 0.0 copy-done
  257.2 0.0 copy-done.1
  257.2 0.6 convolution_subtract_fusion.1
  257.8 0.6 fusion.22
  258.4 32.8 %convolution_subtract_fusion = f32[4096,2048]{1,0:T(8,128)} fusion(f32[4096,2048]{1,0:T(8,128)} %param.2, f32[64,4096]{1,0:T(8,128)S(1)} %select_select_fusion, f32[64,4096]{1,0:T(8,128)S(1)} %fusion.19, f32[64,2048]{1,0:T(8,128)S(1)} %fusion.22, f32[64,2048]{1,0:T(8,128)S(1)} %copy-done), kind=kOutput, calls=%fused_computation.1 | convolution fusion | flops 12894076928 | bytes 70254592 | tf_op jit(solution)/shard_map/dot_general | solution.py:15
  (4 shorter events, 0.0 us)
Async XLA Ops:
  6.5 33.1 %all-gather.2.cloned.1.call-start = ((), (), s32[]{:S(2)}) async-start(), calls=%async_computation | async-start | bytes 1310720 | tf_op jit(solution)/shard_map/all_gather | solution.py:42
  7.3 128.2 %all-reduce.6.cloned.1.call-start = ((), (), s32[]{:S(2)}) async-start(), calls=%async_computation.2 | async-start | bytes 2097152 | tf_op jit(solution)/shard_map/psum | solution.py:11
  85.2 152.6 %all-reduce.4.cloned.1.call-start = ((), (), s32[]{:S(2)}) async-start(), calls=%async_computation.1 | async-start | bytes 2097152 | tf_op jit(solution)/shard_map/psum | solution.py:54
  135.4 121.8 %copy-start = (f32[64,2048]{1,0:T(8,128)S(1)}, f32[64,2048]{1,0:T(8,128)}, u32[]{:S(2)}) copy-start(f32[64,2048]{1,0:T(8,128)} %get-tuple-element.5) | copy-start | bytes 1572868
  135.4 121.8 %copy-start.1 = (f32[64,2048]{1,0:T(8,128)S(1)}, f32[64,2048]{1,0:T(8,128)}, u32[]{:S(2)}) copy-start(f32[64,2048]{1,0:T(8,128)} %get-tuple-element.6) | copy-start | bytes 1572868
Sparse Core Ops, SparseCore 0:
  8.9 30.6 all-gather.1
  85.3 50.0 all-reduce.5
  178.4 59.3 all-reduce.3
where the time goes:
time: 298 us
  waiting for transfers between devices  141 us (47%)
  matrix products  108 us (36%)
  blocking collectives  32.4 us (11%)
  between operations  13.3 us (4%)
    dot_general x7, matrix products, contract(): return lax.dot_general(left, right, (dims, ((), ())), precision=highest)  105 us
    psum x1, waiting for transfers between devices, on_device(): summed = lax.psum(partial_value, ('col', 'dep'))  59 us
    psum x1, waiting for transfers between devices, broadcast(): return lax.psum(kept, axis)  49.1 us
    all_gather x1, waiting for transfers between devices, on_device(): gathered = lax.all_gather(vectors, 'col', axis=1, tiled=True)  32.3 us
    psum x1, blocking collectives, on_device(): gram_total, first_total = lax.psum((gram_part, first_part), 'row')  16.2 us
    psum x1, blocking collectives, on_device(): cross_term = lax.psum(contract(row_vectors, update, ((1,), (1,))), 'row')  16.2 us
  transfers between devices with their start and end apart: 3, of which 3 were waited for; matrix products, arithmetic and copies ran while one was open for 0% of the time, Pallas kernels for 0%

commit v1 on v0

--- a/solution.py
+++ b/solution.py
@@ -1,9 +1,25 @@
+import functools
 import jax
 import jax.numpy as jnp
 from jax import lax
 from jax.sharding import PartitionSpec as P
 
 highest = lax.Precision.HIGHEST
+
+
+def connect_the_loops(message, array_dim):
+    axis_total = lax.axis_size("col")
+    right_arr = sorted(((tick, (tick + 1) % axis_total) for tick in range(axis_total)))
+    prior = message
+    xs_all = [prior]
+    for k0 in range(1, axis_total):
+        prior = lax.ppermute(prior, "col", right_arr)
+        xs_all.insert(0, prior)
+    main = jnp.concatenate(xs_all, array_dim)
+    return jnp.roll(main, (lax.axis_index("col") + 1) * message.shape[array_dim], array_dim)
+
+
+update_vectors_over_axis = functools.partial(connect_the_loops, array_dim=1)
 
 
 def broadcast(value, axis, source):
@@ -39,7 +55,7 @@
 def on_device(matrix, vectors):
     rows_dev, cols_dev = matrix.shape
     row_index = lax.axis_index("row")
-    gathered = lax.all_gather(vectors, "col", axis=1, tiled=True)
+    gathered = update_vectors_over_axis(vectors)
     row_vectors = mask_vectors(gathered, row_index * rows_dev)
     col_block = lax.axis_index("col") * lax.axis_size("dep") + lax.axis_index("dep")
     offset = col_block * cols_dev - row_index * rows_dev

time: 298 us -> 289 us (0.970)
  waiting for transfers between devices: 141 us -> 133 us
  matrix products: 108 us -> 103 us
  starting transfers between devices: 0.26 us -> 3.28 us
    all_gather x1 -> x0, waiting for transfers between devices: 32.3 us -> none  [on_device(): gathered = lax.all_gather(vectors, 'col', axis=1, tiled=True)]
    ppermute x0 -> x3, waiting for transfers between devices: none -> 26.3 us  [connect_the_loops(): prior = lax.ppermute(prior, 'col', right_arr)]
    dot_general x7, matrix products: 105 us -> 101 us  [contract(): return lax.dot_general(left, right, (dims, ((), ())), precision=highest)]
    ppermute x0 -> x3, starting transfers between devices: none -> 3.06 us  [connect_the_loops(): prior = lax.ppermute(prior, 'col', right_arr)]
  transfers between devices with their start and end apart: 3 -> 5, of which waited for: 3 -> 5; matrix products, arithmetic and copies ran while one was open for 0% -> 0% of each run, Pallas kernels for 0% -> 0%
where the time goes in v1:
time: 289 us; the launch traced here: 288 us
  waiting for transfers between devices  133 us (46%)
  matrix products  103 us (36%)
  blocking collectives  32.2 us (11%)
  between operations  13.6 us (5%)
  starting transfers between devices  3.28 us (1%)
    dot_general x7, matrix products, contract(): return lax.dot_general(left, right, (dims, ((), ())), precision=highest)  101 us
    psum x1, waiting for transfers between devices, on_device(): summed = lax.psum(partial_value, ('col', 'dep'))  59 us
    psum x1, waiting for transfers between devices, broadcast(): return lax.psum(kept, axis)  47.8 us
    ppermute x3, waiting for transfers between devices, connect_the_loops(): prior = lax.ppermute(prior, 'col', right_arr)  26.3 us
    psum x1, blocking collectives, on_device(): cross_term = lax.psum(contract(row_vectors, update, ((1,), (1,))), 'row')  16.2 us
    psum x1, blocking collectives, on_device(): gram_total, first_total = lax.psum((gram_part, first_part), 'row')  16 us
  transfers between devices with their start and end apart: 5, of which 5 were waited for; matrix products, arithmetic and copies ran while one was open for 0% of the time, Pallas kernels for 0%

profile of v1, /device:TPU:0, one launch (start us, length us, event | category | flops | bytes accessed | tf_op | source)
XLA Modules:
  0.0 288.3 jit_solution(6949529960868423192)
XLA Ops:
  6.5 0.0 copy-start.1
  6.5 0.0 all-reduce.6.cloned.1.call-start
  6.5 3.1 %collective-permute-start = (f32[64,1024]{1,0:T(8,128)}, f32[64,1024]{1,0:T(8,128)S(1)}, u32[]{:S(2)}, u32[]{:S(2)}) collective-permute-start(f32[64,1024]{1,0:T(8,128)} %param.3), channel_id=1, source_target_pairs={{0,2},{2,4},{4,6},{6,0},{1,3},{3,5},{5,7},{7,1},{8,10},{10,12},{12... | collective-permute-start | bytes 786440 | tf_op jit(solution)/shard_map/ppermute | solution.py:16
  9.6 8.6 %collective-permute-done = f32[64,1024]{1,0:T(8,128)S(1)} collective-permute-done((f32[64,1024]{1,0:T(8,128)}, f32[64,1024]{1,0:T(8,128)S(1)}, u32[]{:S(2)}, u32[]{:S(2)}) %collective-permute-start) | collective-permute-done | bytes 262176 | tf_op jit(solution)/shard_map/ppermute | solution.py:16
  18.2 0.0 collective-permute-start.1
  18.2 9.3 %collective-permute-done.1 = f32[64,1024]{1,0:T(8,128)S(1)} collective-permute-done((f32[64,1024]{1,0:T(8,128)S(1)}, f32[64,1024]{1,0:T(8,128)S(1)}, u32[]{:S(2)}, u32[]{:S(2)}) %collective-permute-start.1) | collective-permute-done | bytes 262176 | tf_op jit(solution)/shard_map/ppermute | solution.py:16
  27.5 0.0 collective-permute-start.2
  27.5 8.4 %collective-permute-done.2 = f32[64,1024]{1,0:T(8,128)S(1)} collective-permute-done((f32[64,1024]{1,0:T(8,128)S(1)}, f32[64,1024]{1,0:T(8,128)S(1)}, u32[]{:S(2)}, u32[]{:S(2)}) %collective-permute-start.2) | collective-permute-done | bytes 262176 | tf_op jit(solution)/shard_map/ppermute | solution.py:16
  36.0 1.0 constant_dynamic-update-slice_fusion.4
  37.0 0.0 copy-done.1
  37.1 0.2 select_select_fusion
  37.3 1.0 fusion.14
  38.2 16.0 %psum.35 = f32[64,64]{1,0:T(8,128)S(1)} all-reduce(f32[64,64]{1,0:T(8,128)S(1)} %fusion.14), channel_id=1, replica_groups=mesh['row'=4,'col'=4,'dep'=2] {'row'}, use_global_device_ids=true, to_apply=%region_0.1 | all-reduce | flops 4096 | bytes 32768 | tf_op jit(solution)/shard_map/psum | solution.py:67
  54.2 0.8 gather_fusion
  55.1 0.2 fusion.10
  55.3 0.2 fusion.15
  55.5 24.8 %fusion.20 = f32[64,2048]{1,0:T(8,128)} fusion(f32[64,4096]{1,0:T(8,128)S(1)} %select_select_fusion, f32[4096,2048]{1,0:T(8,128)} %param.2), kind=kOutput, calls=%fused_computation.47 | convolution fusion | flops 6442450944 | bytes 35127296 | tf_op jit(solution)/shard_map/dot_general | solution.py:31
  80.3 0.8 dynamic-slice_select_fusion
  81.1 0.0 all-reduce.6.cloned.1.call-update
  81.2 0.2 all-reduce.4.cloned.1.call-start
  81.4 0.2 fusion.16
  81.5 0.2 fusion.6
  81.8 0.2 fusion.7
  82.0 0.2 fusion.17
  82.1 0.2 fusion.8
  82.3 47.8 %all-reduce.6.cloned.1.call-done = (f32[64,2048]{1,0:T(8,128)}, f32[64,2048]{1,0:T(8,128)}) async-done(((f32[64,2048]{1,0:T(8,128)}, f32[64,2048]{1,0:T(8,128)}), (f32[64,2048]{1,0:T(8,128)}, f32[64,2048]{1,0:T(8,128)})) %all-reduce.6.cloned.1.call-update) | async-done | bytes 1048592 | tf_op jit(solution)/shard_map/psum | solution.py:27
  130.2 38.3 %fusion.18 = f32[64,4096]{1,0:T(8,128)} fusion(f32[64,2048]{1,0:T(8,128)} %get-tuple-element.5, f32[4096,2048]{1,0:T(8,128)} %param.2), kind=kOutput, calls=%fused_computation.45 | convolution fusion | flops 6442450944 | bytes 35127296 | tf_op jit(solution)/shard_map/dot_general | solution.py:31
  168.4 0.0 all-reduce.4.cloned.1.call-update
  168.4 0.2 convolution_add_fusion
  168.6 0.2 fusion.9
  168.8 0.2 convolution_divide_fusion
  169.0 0.0 copy-start
  169.0 0.0 copy-start.2
  169.0 59.0 %all-reduce.4.cloned.1.call-done = f32[64,4096]{1,0:T(8,128)} async-done(((f32[64,4096]{1,0:T(8,128)}), f32[64,4096]{1,0:T(8,128)}) %all-reduce.4.cloned.1.call-update) | async-done | bytes 1048592 | tf_op jit(solution)/shard_map/psum | solution.py:70
  227.9 2.2 fusion.19
  230.2 1.0 fusion.21
  231.2 16.2 %psum.39 = f32[64,64]{1,0:T(8,128)S(1)} all-reduce(f32[64,64]{1,0:T(8,128)S(1)} %fusion.21), channel_id=1, replica_groups=mesh['row'=4,'col'=4,'dep'=2] {'row'}, use_global_device_ids=true, to_apply=%region_4.5 | all-reduce | flops 4096 | bytes 32768 | tf_op jit(solution)/shard_map/psum | solution.py:72
  247.4 0.0 copy-done
  247.4 0.0 copy-done.2
  247.4 0.6 convolution_subtract_fusion.1
  248.0 0.6 fusion.22
  248.6 32.8 %convolution_subtract_fusion = f32[4096,2048]{1,0:T(8,128)} fusion(f32[4096,2048]{1,0:T(8,128)} %param.2, f32[64,4096]{1,0:T(8,128)S(1)} %select_select_fusion, f32[64,4096]{1,0:T(8,128)S(1)} %fusion.19, f32[64,2048]{1,0:T(8,128)S(1)} %fusion.22, f32[64,2048]{1,0:T(8,128)S(1)} %copy-done), kind=kOutput, calls=%fused_computation.1 | convolution fusion | flops 12894076928 | bytes 70254592 | tf_op jit(solution)/shard_map/dot_general | solution.py:31
  (11 shorter events, 0.2 us)
Async XLA Ops:
  6.5 30.5 %copy-start.1 = (f32[64,1024]{1,0:T(8,128)S(1)}, f32[64,1024]{1,0:T(8,128)}, u32[]{:S(2)}) copy-start(f32[64,1024]{1,0:T(8,128)} %param.3) | copy-start | bytes 786436
  6.5 123.6 %all-reduce.6.cloned.1.call-start = ((), (), s32[]{:S(2)}) async-start(), calls=%async_computation.1 | async-start | bytes 2097152 | tf_op jit(solution)/shard_map/psum | solution.py:27
  6.5 11.7 %collective-permute-start = (f32[64,1024]{1,0:T(8,128)}, f32[64,1024]{1,0:T(8,128)S(1)}, u32[]{:S(2)}, u32[]{:S(2)}) collective-permute-start(f32[64,1024]{1,0:T(8,128)} %param.3), channel_id=1, source_target_pairs={{0,2},{2,4},{4,6},{6,0},{1,3},{3,5},{5,7},{7,1},{8,10},{10,12},{12... | collective-permute-start | bytes 786440 | tf_op jit(solution)/shard_map/ppermute | solution.py:16
  18.2 9.3 %collective-permute-start.1 = (f32[64,1024]{1,0:T(8,128)S(1)}, f32[64,1024]{1,0:T(8,128)S(1)}, u32[]{:S(2)}, u32[]{:S(2)}) collective-permute-start(f32[64,1024]{1,0:T(8,128)S(1)} %collective-permute-done), channel_id=1, source_target_pairs={{0,2},{2,4},{4,6},{6,0},{1,3},{3,5},{5,7},{7,1},{8,10},{10,12},{12... | collective-permute-start | bytes 786440 | tf_op jit(solution)/shard_map/ppermute | solution.py:16
  27.5 8.4 %collective-permute-start.2 = (f32[64,1024]{1,0:T(8,128)S(1)}, f32[64,1024]{1,0:T(8,128)S(1)}, u32[]{:S(2)}, u32[]{:S(2)}) collective-permute-start(f32[64,1024]{1,0:T(8,128)S(1)} %collective-permute-done.1), channel_id=1, source_target_pairs={{0,2},{2,4},{4,6},{6,0},{1,3},{3,5},{5,7},{7,1},{8,10},{10,12},{12... | collective-permute-start | bytes 786440 | tf_op jit(solution)/shard_map/ppermute | solution.py:16
  81.2 146.8 %all-reduce.4.cloned.1.call-start = ((), (), s32[]{:S(2)}) async-start(), calls=%async_computation | async-start | bytes 2097152 | tf_op jit(solution)/shard_map/psum | solution.py:70
  169.0 78.4 %copy-start = (f32[64,2048]{1,0:T(8,128)S(1)}, f32[64,2048]{1,0:T(8,128)}, u32[]{:S(2)}) copy-start(f32[64,2048]{1,0:T(8,128)} %get-tuple-element.5) | copy-start | bytes 1572868
  169.0 78.4 %copy-start.2 = (f32[64,2048]{1,0:T(8,128)S(1)}, f32[64,2048]{1,0:T(8,128)}, u32[]{:S(2)}) copy-start(f32[64,2048]{1,0:T(8,128)} %get-tuple-element.6) | copy-start | bytes 1572868
Sparse Core Ops, SparseCore 0:
  81.3 48.8 all-reduce.5
  168.6 59.3 all-reduce.3

commit v2 on v0

--- a/solution.py
+++ b/solution.py
@@ -8,7 +8,8 @@
 
 def broadcast(value, axis, source):
     kept = jnp.where(lax.axis_index(axis) == source, value, 0).astype(value.dtype)
-    return lax.psum(kept, axis)
+    lift_notes = lambda arr_in, ax_name: jnp.sum(jax.lax.all_gather(arr_in, ax_name), axis=0)
+    return lift_notes(kept, axis)
 
 
 def contract(left, right, dims):

time: 298 us -> 279 us (0.936)
  waiting for transfers between devices: 141 us -> 125 us
  matrix products: 108 us -> 102 us
    psum x1, waiting for transfers between devices: 49.1 us -> 28 us  [on_device(): gram_total, first_total = lax.psum((gram_part, first_part), 'row')]
    dot_general x7, matrix products: 105 us -> 99 us  [contract(): return lax.dot_general(left, right, (dims, ((), ())), precision=highest)]
    all_gather x0 -> x1, waiting for transfers between devices: none -> 5.55 us  [broadcast(): jax.lax.all_gather(arr_in, ax_name)]
  transfers between devices with their start and end apart: 3 -> 4, of which waited for: 3 -> 4; matrix products, arithmetic and copies ran while one was open for 0% -> 11% of each run, Pallas kernels for 0% -> 0%
where the time goes in v2:
time: 279 us
  waiting for transfers between devices  125 us (45%)
  matrix products  102 us (37%)
  blocking collectives  32.6 us (12%)
  between operations  13.3 us (5%)
  other arithmetic  4.05 us (1%)
    dot_general x7, matrix products, contract(): return lax.dot_general(left, right, (dims, ((), ())), precision=highest)  99 us
    psum x1, waiting for transfers between devices, on_device(): summed = lax.psum(partial_value, ('col', 'dep'))  58.6 us
    all_gather x1, waiting for transfers between devices, on_device(): gathered = lax.all_gather(vectors, 'col', axis=1, tiled=True)  32.3 us
    psum x1, waiting for transfers between devices, on_device(): gram_total, first_total = lax.psum((gram_part, first_part), 'row')  28 us
    psum x1, blocking collectives, on_device(): cross_term = lax.psum(contract(row_vectors, update, ((1,), (1,))), 'row')  16.4 us
    psum x1, blocking collectives, on_device(): gram_total, first_total = lax.psum((gram_part, first_part), 'row')  16.2 us
  transfers between devices with their start and end apart: 4, of which 4 were waited for; matrix products, arithmetic and copies ran while one was open for 11% of the time, Pallas kernels for 0%

profile of v2, /device:TPU:0, one launch (start us, length us, event | category | flops | bytes accessed | tf_op | source)
XLA Modules:
  0.0 278.8 jit_solution(10524966903585591171)
XLA Ops:
  6.5 0.0 all-gather.4.cloned.1.call-start
  6.5 0.7 all-gather.4.cloned.1.call-update
  7.3 0.0 all-gather.6.cloned.1.call-start
  7.4 32.3 %all-gather.4.cloned.1.call-done = f32[64,4096]{1,0:T(8,128)} async-done(((f32[64,1024]{1,0:T(8,128)}), f32[64,4096]{1,0:T(8,128)}) %all-gather.4.cloned.1.call-update) | async-done | bytes 1048592 | tf_op jit(solution)/shard_map/all_gather | solution.py:43
  39.6 1.4 select_select_fusion
  41.1 1.0 fusion.14
  42.0 16.2 %psum.28 = f32[64,64]{1,0:T(8,128)S(1)} all-reduce(f32[64,64]{1,0:T(8,128)S(1)} %fusion.14), channel_id=1, replica_groups=mesh['row'=4,'col'=4,'dep'=2] {'row'}, use_global_device_ids=true, to_apply=%region_0.1 | all-reduce | flops 4096 | bytes 32768 | tf_op jit(solution)/shard_map/psum | solution.py:52
  58.3 0.8 dynamic-slice_select_fusion
  59.1 0.0 all-gather.6.cloned.1.call-update
  59.2 0.0 all-reduce.3.cloned.1.call-start
  59.2 0.8 gather_fusion
  60.0 0.2 fusion.10
  60.3 0.2 fusion.15
  60.4 0.2 fusion.16
  60.6 0.2 fusion.6
  60.8 0.2 fusion.7
  61.0 0.2 fusion.17
  61.2 0.2 fusion.8
  61.4 25.2 %fusion.20 = f32[64,2048]{1,0:T(8,128)} fusion(f32[64,4096]{1,0:T(8,128)S(1)} %select_select_fusion, f32[4096,2048]{1,0:T(8,128)} %param.2), kind=kOutput, calls=%fused_computation.39 | convolution fusion | flops 6442450944 | bytes 35127296 | tf_op jit(solution)/shard_map/dot_general | solution.py:16
  86.5 5.5 %all-gather.6.cloned.1.call-done = f32[256,2048]{1,0:T(8,128)} async-done(((f32[64,2048]{1,0:T(8,128)}), f32[256,2048]{1,0:T(8,128)}) %all-gather.6.cloned.1.call-update) | async-done | bytes 2097168 | tf_op jit(solution)/shard_map/all_gather | solution.py:11
  92.1 1.8 reduce_sum.9
  93.8 36.2 %fusion.18 = f32[64,4096]{1,0:T(8,128)} fusion(f32[64,2048]{1,0:T(8,128)S(1)} %reduce_sum.9, f32[4096,2048]{1,0:T(8,128)} %param.2), kind=kOutput, calls=%fused_computation.37 | convolution fusion | flops 6442450944 | bytes 35127296 | tf_op jit(solution)/shard_map/dot_general | solution.py:16
  130.0 0.0 all-reduce.3.cloned.1.call-update
  130.1 0.2 all-reduce.5.cloned.1.call-start
  130.3 0.2 convolution_add_fusion
  130.5 0.2 fusion.9
  130.6 0.2 convolution_divide_fusion
  130.8 0.0 all-reduce.5.cloned.1.call-update
  130.8 58.6 %all-reduce.3.cloned.1.call-done = f32[64,4096]{1,0:T(8,128)} async-done(((f32[64,4096]{1,0:T(8,128)}), f32[64,4096]{1,0:T(8,128)}) %all-reduce.3.cloned.1.call-update) | async-done | bytes 1048592 | tf_op jit(solution)/shard_map/psum | solution.py:55
  189.5 2.2 fusion.19
  191.7 1.0 fusion.21
  192.7 16.4 %psum.31 = f32[64,64]{1,0:T(8,128)S(1)} all-reduce(f32[64,64]{1,0:T(8,128)S(1)} %fusion.21), channel_id=1, replica_groups=mesh['row'=4,'col'=4,'dep'=2] {'row'}, use_global_device_ids=true, to_apply=%region_4.5 | all-reduce | flops 4096 | bytes 32768 | tf_op jit(solution)/shard_map/psum | solution.py:57
  209.1 28.0 %all-reduce.5.cloned.1.call-done = f32[64,2048]{1,0:T(8,128)} async-done(((f32[64,2048]{1,0:T(8,128)}), f32[64,2048]{1,0:T(8,128)}) %all-reduce.5.cloned.1.call-update) | async-done | bytes 524304 | tf_op jit(solution)/shard_map/psum | solution.py:52
  237.1 1.6 convolution_subtract_fusion.1
  238.8 0.6 fusion.22
  239.4 32.9 %convolution_subtract_fusion = f32[4096,2048]{1,0:T(8,128)} fusion(f32[4096,2048]{1,0:T(8,128)} %param.2, f32[64,4096]{1,0:T(8,128)S(1)} %select_select_fusion, f32[64,4096]{1,0:T(8,128)S(1)} %fusion.19, f32[64,2048]{1,0:T(8,128)S(1)} %fusion.22, f32[64,2048]{1,0:T(8,128)S(1)} %reduce_sum.9), kind=kOutput, calls=%fused_computation.1 | convolution fusion | flops 12894076928 | bytes 70254592 | tf_op jit(solution)/shard_map/dot_general | solution.py:16
  (4 shorter events, 0.0 us)
Async XLA Ops:
  6.5 33.1 %all-gather.4.cloned.1.call-start = ((), (), s32[]{:S(2)}) async-start(), calls=%async_computation | async-start | bytes 1310720 | tf_op jit(solution)/shard_map/all_gather | solution.py:43
  7.3 84.8 %all-gather.6.cloned.1.call-start = ((), (), s32[]{:S(2)}) async-start(), calls=%async_computation.3 | async-start | bytes 2621440 | tf_op jit(solution)/shard_map/all_gather | solution.py:11
  59.2 130.3 %all-reduce.3.cloned.1.call-start = ((), (), s32[]{:S(2)}) async-start(), calls=%async_computation.1 | async-start | bytes 2097152 | tf_op jit(solution)/shard_map/psum | solution.py:55
  130.1 107.1 %all-reduce.5.cloned.1.call-start = ((), (), s32[]{:S(2)}) async-start(), calls=%async_computation.2 | async-start | bytes 1048576 | tf_op jit(solution)/shard_map/psum | solution.py:52
Sparse Core Ops, SparseCore 0:
  8.9 30.6 all-gather.3
  59.3 32.7 all-gather.5
  130.2 59.2 all-reduce.2
  192.3 44.7 all-reduce.4
